TPU v7x, 256 devices: a whole 4x4x8 slice. The times are simulated.
256 devices in a mesh: pair: 16 (over y_hi, x, core), tile: 16 (over y_lo, z).
Axes of the slice: x: 4, y: 4 (y_hi: 2, y_lo: 2; y = y_hi * 2 + y_lo), z: 8, core: 2. Of those that a mesh axis runs over, the one named last changes fastest.
Arguments:
- fixed: float32 [32768, 2048], P('pair', 'tile'), parts along dimension 0, may hold values from -6 to 6
- moving: float32 [32768, 2048], P('pair', 'tile'), parts along dimension 0, may hold values from -6 to 6
- offsets: int32 [2, 32768, 2048], P(None, ('pair', 'tile')), parts along dimension 1, may hold values from -3 to 3
- fractions: float32 [2, 32768, 2048], P(None, ('pair', 'tile')), parts along dimension 1, may hold values from 0 to 1
Outputs:
- warped: float32 [32768, 2048], P(('pair', 'tile')), parts along dimension 0
There are 16 independent parts, one for each index of `pair`. A program takes and returns all parts, laid end to end along the dimension named above; each array names one. Nothing has to cross between parts.
All inputs are finite; a program needn't handle non-finite values.
Results may differ from a plain program's by a relative error of at most 0.00002.
Values sent between devices are 32-bit elements; how exact they have to be, the bound alone decides.
A program may use at most 64 MiB of HBM per device.

v0:
```python
import jax
import jax.numpy as jnp
from jax import lax
from jax.sharding import PartitionSpec as P

RADIUS = 4
REACH = 3


def extended_2(block, sides, width):
    for axis, dim in sides:
        count = lax.axis_size(axis)
        forward = [(i, i + 1) for i in range(count - 1)]
        backward = [(target, source) for source, target in forward]
        low = lax.ppermute(
            lax.slice_in_dim(block, block.shape[dim] - width, None, axis=dim), axis, forward
        )
        high = lax.ppermute(lax.slice_in_dim(block, 0, width, axis=dim), axis, backward)
        block = jnp.concatenate([low, block, high], axis=dim)
    return block


def window_sum(extended):
    row_total = extended.shape[0] - 2 * RADIUS
    column_total = extended.shape[1] - 2 * RADIUS
    rows_summed = extended[0:row_total, :]
    for shift in range(1, 2 * RADIUS + 1):
        rows_summed = rows_summed + extended[shift : shift + row_total, :]
    result = rows_summed[:, 0:column_total]
    for shift in range(1, 2 * RADIUS + 1):
        result = result + rows_summed[:, shift : shift + column_total]
    return result


def similarity(fixed_ext, moving_ext):
    window_count = float((2 * RADIUS + 1) ** 2)
    fixed_sum = window_sum(fixed_ext)
    moving_sum = window_sum(moving_ext)
    fixed_square = window_sum(fixed_ext * fixed_ext)
    moving_square = window_sum(moving_ext * moving_ext)
    cross_sum = window_sum(fixed_ext * moving_ext)
    fixed_var = fixed_square - fixed_sum * fixed_sum / window_count
    moving_var = moving_square - moving_sum * moving_sum / window_count
    covariance = cross_sum - fixed_sum * moving_sum / window_count
    correlation = covariance / jnp.sqrt(fixed_var * moving_var + 0.001)
    return 0.5 * (1.0 + correlation)


def sample_corners(padded, offsets, band_rows, column_total, margin):
    zeros = jnp.zeros((band_rows, column_total), jnp.float32)
    left_rows = []
    right_rows = []
    for row_shift in range(-REACH, REACH + 2):
        slab = padded[margin + row_shift : margin + row_shift + band_rows, :]
        left_pick = zeros
        right_pick = zeros
        for col_shift in range(-REACH, REACH + 1):
            chosen = offsets[1] == col_shift
            start = margin + col_shift
            left_pick = jnp.where(chosen, slab[:, start : start + column_total], left_pick)
            right_pick = jnp.where(
                chosen, slab[:, start + 1 : start + 1 + column_total], right_pick
            )
        left_rows.append(left_pick)
        right_rows.append(right_pick)
    top_left, top_right, bottom_left, bottom_right = (zeros, zeros, zeros, zeros)
    for row_shift in range(-REACH, REACH + 1):
        chosen = offsets[0] == row_shift
        place = row_shift + REACH
        top_left = jnp.where(chosen, left_rows[place], top_left)
        top_right = jnp.where(chosen, right_rows[place], top_right)
        bottom_left = jnp.where(chosen, left_rows[place + 1], bottom_left)
        bottom_right = jnp.where(chosen, right_rows[place + 1], bottom_right)
    return (top_left, top_right, bottom_left, bottom_right)


def on_device(fixed, moving, offsets, fractions):
    margin = REACH + 1
    band_rows = offsets.shape[1]
    column_total = offsets.shape[2]
    depth = max(RADIUS, margin)
    banded = lax.all_to_all(
        jnp.stack((fixed, moving)), "tile", split_axis=1, concat_axis=2, tiled=True
    )
    deepened = extended_2(banded, (("tile", 1),), depth)
    window_rows = deepened
    window_rows = jnp.pad(window_rows, ((0, 0), (0, 0), (RADIUS, RADIUS)))
    confidence = similarity(window_rows[0], window_rows[1])
    moving_rows = deepened[1, depth - margin : depth + band_rows + margin, :]
    padded = jnp.pad(moving_rows, ((0, 0), (margin, margin)))
    top_left, top_right, bottom_left, bottom_right = sample_corners(
        padded, offsets, band_rows, column_total, margin
    )
    row_weight = confidence * fractions[0]
    column_weight = confidence * fractions[1]
    upper = (1.0 - column_weight) * top_left + column_weight * top_right
    lower = (1.0 - column_weight) * bottom_left + column_weight * bottom_right
    return (1.0 - row_weight) * upper + row_weight * lower


def solution(mesh):
    placed = (
        P("pair", "tile"),
        P("pair", "tile"),
        P(None, ("pair", "tile"), None),
        P(None, ("pair", "tile"), None),
    )
    return jax.shard_map(
        on_device, mesh=mesh, in_specs=placed, out_specs=P(("pair", "tile"), None), check_vma=False
    )
```

profile of v0, /device:TPU:36, one launch (start us, length us, event | category | flops | bytes accessed | tf_op | source)
XLA Modules:
  0.0 121.1 jit_solution(3653359728250834409)
XLA Ops:
  0.0 3.1 %pad_maximum_fusion.1 = f32[2,2048,128]{2,0,1:T(2,128)S(1)} fusion(f32[1,2048,128]{2,0,1:T(1,128)} %bitcast.109, f32[1,2048,128]{2,0,1:T(1,128)} %bitcast.110), kind=kLoop, calls=%fused_computation.5 | loop fusion | flops 524288 | bytes 4194304 | tf_op jit(solution)/shard_map/stack | solution.py:83
  3.1 58.1 %all_to_all.18 = f32[2,2048,128]{2,0,1:T(2,128)S(1)} all-to-all(f32[2,2048,128]{2,0,1:T(2,128)S(1)} %pad_maximum_fusion.1), channel_id=1, replica_groups=mesh['pair'=16,'tile'=16] {'tile'}, dimensions={1} | all-to-all | bytes 4194304 | tf_op jit(solution)/shard_map/all_to_all | solution.py:82
  61.2 1.3 %copy-done.2 = f32[2,2048,128]{2,0,1:T(2,128)} copy-done((f32[2,2048,128]{2,0,1:T(2,128)}, f32[2,2048,128]{2,0,1:T(2,128)S(1)}, u32[]{:S(2)}) %copy-start.2) | copy-done | bytes 2097176
  62.5 2.6 %copy.6 = f32[2,128,16,128]{3,2,1,0:T(8,128)} copy(f32[2,128,16,128]{3,0,1,2:T(2,128)S(1)} %bitcast.106) | data formatting | bytes 4194304 | tf_op jit(solution)/shard_map/all_to_all | solution.py:82
  65.1 1.7 %all_to_all.16 = f32[2,128,2048]{2,1,0:T(8,128)S(1)} reshape(f32[2,128,16,128]{3,2,1,0:T(8,128)} %copy.6) | data formatting | bytes 4194304 | tf_op jit(solution)/shard_map/all_to_all | solution.py:82
  66.8 0.0 copy-start
  66.9 3.0 %collective-permute-start = (f32[2,4,2048]{2,1,0:T(4,128)S(1)}, f32[2,4,2048]{2,1,0:T(4,128)S(1)}, u32[]{:S(2)}, u32[]{:S(2)}) collective-permute-start(f32[2,4,2048]{2,1,0:T(4,128)S(1)} %get-tuple-element.10), channel_id=1, source_target_pairs={{0,1},{1,2},{2,3},{3,4},{4,5},{5,6},{6,7},{7,8},{8,9},{9,10},{10,1... | collective-permute-start | bytes 196616 | tf_op jit(solution)/shard_map/ppermute | solution.py:15
  69.9 0.0 copy-start.3
  69.9 3.2 %collective-permute-start.1 = (f32[2,4,2048]{2,1,0:T(4,128)S(1)}, f32[2,4,2048]{2,1,0:T(4,128)S(1)}, u32[]{:S(2)}, u32[]{:S(2)}) collective-permute-start(f32[2,4,2048]{2,1,0:T(4,128)S(1)} %get-tuple-element.11), channel_id=1, source_target_pairs={{1,0},{2,1},{3,2},{4,3},{5,4},{6,5},{7,6},{8,7},{9,8},{10,9},{11,1... | collective-permute-start | bytes 196616 | tf_op jit(solution)/shard_map/ppermute | solution.py:18
  73.0 1.5 %constant_dynamic-update-slice_fusion.1 = f32[2,132,2048]{2,1,0:T(8,128)} fusion(f32[2,128,2048]{2,1,0:T(8,128)S(1)} %all_to_all.16), kind=kLoop, calls=%fused_computation.139 | loop fusion | bytes 4194304
  74.5 1.1 slice.1100
  75.6 1.6 %copy.7 = f32[1,128,16,128]{3,2,1,0:T(8,128)} copy(f32[1,128,16,128]{3,0,1,2:T(1,128)S(1)} %slice.1100) | data formatting | bytes 2097152 | tf_op jit(solution)/shard_map/slice | solution.py:60
  77.2 0.0 collective-permute-done
  77.2 0.0 collective-permute-done.1
  77.2 0.3 pad_maximum_fusion
  77.5 0.0 copy-start.1
  77.5 0.1 slice_bitcast_fusion
  77.6 1.3 %copy-done.1 = f32[2,136,2048]{2,1,0:T(8,128)} copy-done((f32[2,136,2048]{2,1,0:T(8,128)}, f32[2,136,2048]{2,1,0:T(8,128)S(1)}, u32[]{:S(2)}) %copy-start.1) | copy-done | bytes 2228248
  78.8 6.3 %add_bitcast_fusion = (f32[128,2056]{1,0:T(8,128)S(1)}, f32[128,2056]{1,0:T(8,128)S(1)}) fusion(f32[2,136,2048]{2,1,0:T(8,128)S(1)} %pad_maximum_fusion), kind=kLoop, calls=%fused_computation.34 | loop fusion | flops 4210688 | bytes 4333568 | tf_op jit(solution)/shard_map/add | solution.py:28
  85.1 3.5 %fusion.33 = (f32[1,136,2056]{2,1,0:T(8,128)S(1)}, f32[1,136,2056]{2,1,0:T(8,128)S(1)}, f32[1,136,2056]{2,1,0:T(8,128)S(1)}) fusion(f32[2,136,2048]{2,1,0:T(8,128)} %copy-done.1), kind=kLoop, calls=%fused_computation.136 | loop fusion | flops 838848 | bytes 5583616 | tf_op jit(solution)/shard_map/mul | solution.py:41
  88.7 0.8 fusion.2
  89.5 1.6 %fusion = (f32[128,2056]{1,0:T(8,128)S(1)}, f32[128,2056]{1,0:T(8,128)S(1)}) fusion(f32[1,136,2056]{2,1,0:T(8,128)S(1)} %get-tuple-element.9, f32[1,136,2056]{2,1,0:T(8,128)S(1)} %get-tuple-element.8), kind=kLoop, calls=%fused_computation.8 | loop fusion | flops 4210688 | bytes 21053440 | tf_op jit(solution)/shard_map/add | solution.py:28
  91.1 0.7 constant_dynamic-update-slice_fusion
  91.8 29.3 %multiply_add_fusion = f32[128,2048]{1,0:T(8,128)} fusion(f32[2,132,2048]{2,1,0:T(8,128)} %constant_dynamic-update-slice_fusion, f32[16,8,16,128]{3,2,1,0:T(8,128)} %bitcast.108, f32[2,128,2048]{2,1,0:T(8,128)} %copy-done, f32[2,4,2048]{2,1,0:T(4,128)S(1)} %collective-permute-done, f32[136,2048]{1,0:T(8,128)S(1)} %slice_bitcast_fusion, ...), kind=kLoop, calls=%fused_computation.131 | loop fusion | flops 58720256 | bytes 60948480 | tf_op jit(solution)/shard_map/add | solution.py:98
  (4 shorter events, 0.0 us)
Async XLA Ops:
  61.2 1.3 %copy-start.2 = (f32[2,2048,128]{2,0,1:T(2,128)}, f32[2,2048,128]{2,0,1:T(2,128)S(1)}, u32[]{:S(2)}) copy-start(f32[2,2048,128]{2,0,1:T(2,128)S(1)} %all_to_all.18) | copy-start | bytes 6291460
  66.8 10.4 %copy-start = (f32[2,128,2048]{2,1,0:T(8,128)}, f32[2,128,2048]{2,1,0:T(8,128)S(1)}, u32[]{:S(2)}) copy-start(f32[2,128,2048]{2,1,0:T(8,128)S(1)} %all_to_all.16) | copy-start | bytes 6291460
  66.9 10.3 %collective-permute-start = (f32[2,4,2048]{2,1,0:T(4,128)S(1)}, f32[2,4,2048]{2,1,0:T(4,128)S(1)}, u32[]{:S(2)}, u32[]{:S(2)}) collective-permute-start(f32[2,4,2048]{2,1,0:T(4,128)S(1)} %get-tuple-element.10), channel_id=1, source_target_pairs={{0,1},{1,2},{2,3},{3,4},{4,5},{5,6},{6,7},{7,8},{8,9},{9,10},{10,1... | collective-permute-start | bytes 196616 | tf_op jit(solution)/shard_map/ppermute | solution.py:15
  69.9 4.7 %copy-start.3 = (f32[2,2048,128]{2,0,1:T(2,128)S(1)}, f32[2,2048,128]{2,0,1:T(2,128)}, u32[]{:S(2)}) copy-start(f32[2,2048,128]{2,0,1:T(2,128)} %copy-done.2) | copy-start | bytes 6291460
  69.9 7.3 %collective-permute-start.1 = (f32[2,4,2048]{2,1,0:T(4,128)S(1)}, f32[2,4,2048]{2,1,0:T(4,128)S(1)}, u32[]{:S(2)}, u32[]{:S(2)}) collective-permute-start(f32[2,4,2048]{2,1,0:T(4,128)S(1)} %get-tuple-element.11), channel_id=1, source_target_pairs={{1,0},{2,1},{3,2},{4,3},{5,4},{6,5},{7,6},{8,7},{9,8},{10,9},{11,1... | collective-permute-start | bytes 196616 | tf_op jit(solution)/shard_map/ppermute | solution.py:18
  77.5 1.3 %copy-start.1 = (f32[2,136,2048]{2,1,0:T(8,128)}, f32[2,136,2048]{2,1,0:T(8,128)S(1)}, u32[]{:S(2)}) copy-start(f32[2,136,2048]{2,1,0:T(8,128)S(1)} %pad_maximum_fusion) | copy-start | bytes 6684676
where the time goes:
time: 123 us; the launch traced here: 121 us
  blocking collectives  58.1 us (47%)
  other arithmetic  45 us (37%)
  local copies, waits for them, and re-layouts  11.7 us (10%)
  starting transfers between devices  6.15 us (5%)
    all_to_all x1, blocking collectives, on_device(): lax.all_to_all(jnp.stack((fixed, moving)), 'tile', split_axis=1, concat_a...  58.1 us
    add x1, other arithmetic, on_device(): return (1.0 - row_weight) * upper + row_weight * lower  29.3 us
    add x3, other arithmetic, window_sum(): rows_summed = rows_summed + extended[shift:shift + row_total, :]  8.73 us
    all_to_all x2, local copies, waits for them, and re-layouts, on_device(): lax.all_to_all(jnp.stack((fixed, moving)), 'tile', split_axis=1, concat_a...  4.27 us
    unnamed x9, local copies, waits for them, and re-layouts  4.06 us
    mul x1, other arithmetic, similarity(): cross_sum = window_sum(fixed_ext * moving_ext)  3.54 us
    ppermute x1, starting transfers between devices, extended_2(): lax.ppermute(lax.slice_in_dim(block, 0, width, axis=dim), axis, backward)  3.16 us
    another operation x1, other arithmetic, on_device(): jnp.stack((fixed, moving))  3.13 us
  transfers between devices with their start and end apart: 2, of which 0 were waited for; matrix products, arithmetic and copies ran while one was open for 3% of the time, Pallas kernels for 0%

commit v1 on v0

v1 whole, which is shorter than its diff:
```python
import functools

import jax
import jax.numpy as jnp
from jax import lax
from jax.experimental import pallas as pl
from jax.experimental.pallas import tpu as pltpu
from jax.sharding import PartitionSpec as P

RADIUS = 4
REACH = 3
LANES = 128
GROUP = 8
MESH = pl.DeviceIdType.MESH
COLUMN_SHIFTS = tuple(range(-REACH, REACH + 2))
CHUNKS = (2, 2, 2, 2, 2, 2, 2, 1, 1)


def kernel(
    strips,
    near,
    fixed_ref,
    moving_ref,
    offsets_ref,
    fractions_ref,
    out_ref,
    images,
    shifted,
    sums,
    confidences,
    offsets_buf,
    fractions_buf,
    send_sem,
    recv_sem,
    local_sem,
):
    me = lax.axis_index("tile")
    band = out_ref.shape[0]
    last = strips - 1
    moving_at = strips + 2

    barrier = pltpu.get_barrier_semaphore()
    for step in range(1, strips):
        pl.semaphore_signal(
            barrier, inc=1, device_id={"tile": lax.rem(me + step, strips)}, device_id_type=MESH
        )

    def own_copies(source, target, rows):
        return [
            pltpu.make_async_copy(
                ref.at[pl.ds(source, rows)],
                images.at[base + 1 + me, pl.ds(target, rows)],
                local_sem.at[place],
            )
            for place, (ref, base) in enumerate(((fixed_ref, 0), (moving_ref, moving_at)))
        ]

    whole = band + 2 * RADIUS
    first_own = own_copies(0, RADIUS, whole - RADIUS)
    last_own = own_copies(last * band - RADIUS, 0, whole - RADIUS)
    inner_own = own_copies(jnp.clip(me, 1, last - 1) * band - RADIUS, 0, whole)

    def each_own(act):
        @pl.when(me == 0)
        def _():
            for copy in first_own:
                act(copy)

        @pl.when(me == last)
        def _():
            for copy in last_own:
                act(copy)

        @pl.when(jnp.logical_and(me > 0, me < last))
        def _():
            for copy in inner_own:
                act(copy)

    each_own(lambda copy: copy.start())
    offsets_copy = pltpu.make_async_copy(offsets_ref, offsets_buf, local_sem.at[2])
    fractions_copy = pltpu.make_async_copy(fractions_ref, fractions_buf, local_sem.at[3])
    offsets_copy.start()
    fractions_copy.start()

    for base in (0, moving_at):
        for side in (base, base + strips + 1):
            images[side] = jnp.zeros(images.shape[1:], jnp.float32)

        @pl.when(me == 0)
        def _():
            images[pl.ds(base + 1, strips), 0:RADIUS, :] = jnp.zeros(
                (strips, RADIUS, LANES), jnp.float32
            )

        @pl.when(me == last)
        def _():
            images[pl.ds(base + 1, strips), band + RADIUS : whole, :] = jnp.zeros(
                (strips, RADIUS, LANES), jnp.float32
            )

    for side in (0, strips + 1):
        sums[:, side] = jnp.zeros((sums.shape[0],) + sums.shape[2:], jnp.float32)

    starts = [0]
    for groups in CHUNKS:
        starts.append(max(starts[-1], 2 * RADIUS) + GROUP * groups)
    chunks = len(CHUNKS)

    def target_of(step):
        return lax.rem(me + step, strips)

    def send(chunk, target, skip_top, skip_bottom):
        begin = starts[chunk] + (RADIUS if skip_top else 0)
        rows = starts[chunk + 1] - (RADIUS if skip_bottom else 0) - begin
        for ref, base in ((fixed_ref, 0), (moving_ref, moving_at)):
            pltpu.make_async_remote_copy(
                src_ref=ref.at[pl.ds(target * band - RADIUS + begin, rows)],
                dst_ref=images.at[base + 1 + me, pl.ds(begin, rows)],
                send_sem=send_sem.at[chunk],
                recv_sem=recv_sem.at[chunk],
                device_id={"tile": target},
                device_id_type=MESH,
            ).start()

    def count(sem, blocks, rows):
        piece = images.at[pl.ds(0, blocks), pl.ds(0, rows)]
        pltpu.make_async_copy(piece, piece, sem).wait()

    pl.semaphore_wait(barrier, strips - 1)
    for chunk in range(chunks):
        for target in near(me):
            if chunk == 0:
                pl.when(target == 0)(functools.partial(send, chunk, target, True, False))
                pl.when(target != 0)(functools.partial(send, chunk, target, False, False))
            elif chunk == chunks - 1:
                pl.when(target == last)(functools.partial(send, chunk, target, False, True))
                pl.when(target != last)(functools.partial(send, chunk, target, False, False))
            else:
                send(chunk, target, False, False)

    lane = lax.broadcasted_iota(jnp.int32, (GROUP, LANES), 1)

    def from_right(shift, centre, right):
        return pltpu.roll(jnp.where(lane < shift, right, centre), LANES - shift, 1)

    def from_left(shift, centre, left):
        return pltpu.roll(jnp.where(lane >= LANES - shift, left, centre), shift, 1)

    def make_shifted(row):
        def strip_step(strip, carry):
            left, centre, right = (
                images[moving_at + strip + side, pl.ds(row, GROUP), :] for side in range(3)
            )
            place = 0
            for shift in COLUMN_SHIFTS:
                if shift < 0:
                    value = from_left(-shift, centre, left)
                elif shift > 0:
                    value = from_right(shift, centre, right)
                else:
                    continue
                shifted[place, strip, pl.ds(row, GROUP), :] = value
                place += 1
            return carry

        lax.fori_loop(0, strips, strip_step, 0, unroll=2)

    window_count = float((2 * RADIUS + 1) ** 2)

    def row_sums(row):
        def strip_step(strip, carry):
            totals = [None] * 5
            for step in range(2 * RADIUS + 1):
                f = images[strip + 1, pl.ds(row + step, GROUP), :]
                m = images[moving_at + strip + 1, pl.ds(row + step, GROUP), :]
                for place, term in enumerate((f, m, f * f, m * m, f * m)):
                    totals[place] = term if step == 0 else totals[place] + term
            for place, total in enumerate(totals):
                sums[place, strip + 1] = total
            return carry

        lax.fori_loop(0, strips, strip_step, 0, unroll=2)

    def confidence(row):
        def strip_step(strip, carry):
            windows = []
            for place in range(5):
                left, centre, right = (sums[place, strip + side] for side in range(3))
                total = centre
                for shift in range(1, RADIUS + 1):
                    total = total + (
                        from_left(shift, centre, left) + from_right(shift, centre, right)
                    )
                windows.append(total)
            fixed_sum, moving_sum, fixed_square, moving_square, cross_sum = windows
            fixed_var = fixed_square - fixed_sum * fixed_sum * (1.0 / window_count)
            moving_var = moving_square - moving_sum * moving_sum * (1.0 / window_count)
            covariance = cross_sum - fixed_sum * moving_sum * (1.0 / window_count)
            correlation = covariance * lax.rsqrt(fixed_var * moving_var + 0.001)
            confidences[strip] = 0.5 * (1.0 + correlation)
            return carry

        lax.fori_loop(0, strips, strip_step, 0, unroll=2)

    def pick(values, index):
        for bit in (4, 2, 1):
            chosen = jnp.bitwise_and(index, bit) != 0
            values = [
                jnp.where(chosen, values[place + bit], values[place])
                if place + bit < len(values)
                else values[place]
                for place in range(bit + 1)
            ]
        return values

    def warp(row):
        def strip_step(strip, carry):
            here = (pl.ds(row, GROUP), pl.ds(pl.multiple_of(strip * LANES, LANES), LANES))
            row_index = offsets_buf[(0,) + here] + REACH
            column_index = offsets_buf[(1,) + here] + REACH
            weight = confidences[strip]
            row_weight = weight * fractions_buf[(0,) + here]
            column_weight = weight * fractions_buf[(1,) + here]
            other_weight = 1.0 - column_weight
            blended = []
            for row_shift in COLUMN_SHIFTS:
                rows = pl.ds(row + RADIUS + row_shift, GROUP)
                columns = []
                place = 0
                for shift in COLUMN_SHIFTS:
                    if shift == 0:
                        columns.append(images[moving_at + 1 + strip, rows, :])
                    else:
                        columns.append(shifted[place, strip, rows, :])
                        place += 1
                left, right = pick(columns, column_index)
                blended.append(other_weight * left + column_weight * right)
            upper, lower = pick(blended, row_index)
            out_ref[here] = (1.0 - row_weight) * upper + row_weight * lower
            return carry

        lax.fori_loop(0, strips, strip_step, 0)

    done = 0
    for chunk in range(chunks):
        rows = starts[chunk + 1] - starts[chunk]
        blocks = 2 * (strips - 1)
        if chunk == 0 or chunk == chunks - 1:
            edge = 0 if chunk == 0 else last
            pl.when(me == edge)(
                functools.partial(count, recv_sem.at[chunk], blocks, rows - RADIUS)
            )
            pl.when(me != edge)(functools.partial(count, recv_sem.at[chunk], blocks, rows))
        else:
            count(recv_sem.at[chunk], blocks, rows)
        if chunk == 0:
            each_own(lambda copy: copy.wait())
            offsets_copy.wait()
            fractions_copy.wait()
            make_shifted(0)

        def group_step(group, carry):
            row = pl.multiple_of(group * GROUP, GROUP)
            make_shifted(row + GROUP)
            row_sums(row)
            confidence(row)
            warp(row)
            return carry

        lax.fori_loop(done, done + CHUNKS[chunk], group_step, 0)
        done += CHUNKS[chunk]

    for chunk in range(chunks):
        rows = starts[chunk + 1] - starts[chunk]
        blocks = 2 * (strips - 1)
        if chunk == 0 or chunk == chunks - 1:
            edge = 0 if chunk == 0 else last

            @pl.when(me != edge)
            def _():
                count(send_sem.at[chunk], blocks - 2, rows)
                count(send_sem.at[chunk], 2, rows - RADIUS)

            pl.when(me == edge)(functools.partial(count, send_sem.at[chunk], blocks, rows))
        else:
            count(send_sem.at[chunk], blocks, rows)


def solution(mesh):
    strips = mesh.shape["tile"]
    ring = 8

    def near(me):
        z, y = lax.rem(me, ring), me // ring
        steps = [(0, 1)]
        for far in range(1, ring // 2 + 1):
            for sign in (1, -1) if far < ring // 2 else (1,):
                steps += [(sign * far, 0), (sign * far, 1)]
        return [
            lax.rem(z + dz + ring, ring) + ring * lax.rem(y + dy, strips // ring)
            for dz, dy in steps
        ]

    def on_device(fixed, moving, offsets, fractions):
        band, width = offsets.shape[1:]
        padded = band + 2 * RADIUS + GROUP
        chunks = len(CHUNKS)
        return pl.pallas_call(
            functools.partial(kernel, strips, near),
            out_shape=jax.ShapeDtypeStruct((band, width), jnp.float32),
            in_specs=[pl.BlockSpec(memory_space=pl.ANY)] * 4,
            out_specs=pl.BlockSpec(memory_space=pltpu.VMEM),
            scratch_shapes=[
                pltpu.VMEM((2 * (strips + 2), padded, LANES), jnp.float32),
                pltpu.VMEM((2 * REACH + 1, strips, padded, LANES), jnp.float32),
                pltpu.VMEM((5, strips + 2, GROUP, LANES), jnp.float32),
                pltpu.VMEM((strips, GROUP, LANES), jnp.float32),
                pltpu.VMEM(offsets.shape, offsets.dtype),
                pltpu.VMEM(fractions.shape, fractions.dtype),
                pltpu.SemaphoreType.DMA((chunks,)),
                pltpu.SemaphoreType.DMA((chunks,)),
                pltpu.SemaphoreType.DMA((4,)),
            ],
            compiler_params=pltpu.CompilerParams(
                collective_id=0, has_side_effects=True, vmem_limit_bytes=40 * 2**20
            ),
        )(fixed, moving, offsets, fractions)

    placed = (
        P("pair", "tile"),
        P("pair", "tile"),
        P(None, ("pair", "tile"), None),
        P(None, ("pair", "tile"), None),
    )
    return jax.shard_map(
        on_device, mesh=mesh, in_specs=placed, out_specs=P(("pair", "tile"), None), check_vma=False
    )
```

time: 123 us -> 72.7 us (0.59); the launches traced: 121 us -> 72.5 us
  Pallas kernels: 0 us -> 65.9 us
  blocking collectives: 58.1 us -> 0 us
  other arithmetic: 45 us -> 0 us
  starting transfers between devices: 6.15 us -> 0 us
  local copies, waits for them, and re-layouts: 11.7 us -> 6.6 us
    pallas_call x0 -> x1, Pallas kernels: none -> 65.9 us  [on_device(): pl.pallas_call(functools.partial(kernel, strips, near), out_shape=jax.Sha...]
    all_to_all x1 -> x0, blocking collectives: 58.1 us -> none  [on_device(): lax.all_to_all(jnp.stack((fixed, moving)), 'tile', split_axis=1, concat_a...]
    add x4 -> x0, other arithmetic: 38.1 us -> none  [the longest x1 29.3 us: on_device(): return (1.0 - row_weight) * upper + row_weight * lower]
    ppermute x2 -> x0, starting transfers between devices: 6.15 us -> none  [the longest x1 3.16 us: extended_2(): lax.ppermute(lax.slice_in_dim(block, 0, width, axis=dim), axis, backward)]
    all_to_all x2 -> x0, local copies, waits for them, and re-layouts: 4.27 us -> none  [on_device(): lax.all_to_all(jnp.stack((fixed, moving)), 'tile', split_axis=1, concat_a...]
    mul x1 -> x0, other arithmetic: 3.54 us -> none  [similarity(): cross_sum = window_sum(fixed_ext * moving_ext)]
    another operation x1 -> x0, other arithmetic: 3.13 us -> none  [on_device(): jnp.stack((fixed, moving))]
    slice x3 -> x0, local copies, waits for them, and re-layouts: 2.69 us -> none  [the longest x2 2.67 us: sample_corners(): slab[:, start:start + column_total]]
  transfers between devices with their start and end apart: 2 -> 0, of which waited for: 0 -> 0; matrix products, arithmetic and copies ran while one was open for 3% -> 0% of each run, Pallas kernels for 0% -> 0%
where the time goes in v1:
time: 72.7 us; the launch traced here: 72.5 us
  Pallas kernels  65.9 us (91%)
  local copies, waits for them, and re-layouts  6.6 us (9%)
    pallas_call x1, Pallas kernels, on_device(): pl.pallas_call(functools.partial(kernel, strips, near), out_shape=jax.Sha...  65.9 us
    unnamed x9, local copies, waits for them, and re-layouts  6.6 us

profile of v1, /device:TPU:36, one launch (start us, length us, event | category | flops | bytes accessed | tf_op | source)
XLA Modules:
  0.0 72.5 jit_solution(7903855964967233237)
XLA Ops:
  0.0 0.0 copy-start
  0.0 1.6 %copy-done = s32[2,128,2048]{2,1,0:T(8,128)S(1)} copy-done((s32[2,128,2048]{2,1,0:T(8,128)S(1)}, s32[2,128,2048]{2,1,0:T(8,128)}, u32[]{:S(2)}) %copy-start) | copy-done | bytes 2097176
  1.6 0.0 copy-start.1
  1.6 1.6 %copy-done.1 = f32[2,128,2048]{2,1,0:T(8,128)S(1)} copy-done((f32[2,128,2048]{2,1,0:T(8,128)S(1)}, f32[2,128,2048]{2,1,0:T(8,128)}, u32[]{:S(2)}) %copy-start.1) | copy-done | bytes 2097176
  3.2 0.0 copy-start.2
  3.2 1.2 %copy-done.2 = f32[2048,128]{1,0:T(8,128)S(1)} copy-done((f32[2048,128]{1,0:T(8,128)S(1)}, f32[2048,128]{1,0:T(8,128)}, u32[]{:S(2)}) %copy-start.2) | copy-done | bytes 1048600
  4.4 0.0 copy-start.3
  4.4 1.2 %copy-done.3 = f32[2048,128]{1,0:T(8,128)S(1)} copy-done((f32[2048,128]{1,0:T(8,128)S(1)}, f32[2048,128]{1,0:T(8,128)}, u32[]{:S(2)}) %copy-start.3) | copy-done | bytes 1048600
  5.6 65.9 %shard_map.46 = f32[128,2048]{1,0:T(8,128)S(1)} custom-call(f32[2048,128]{1,0:T(8,128)S(1)} %copy-done.2, f32[2048,128]{1,0:T(8,128)S(1)} %copy-done.3, s32[2,128,2048]{2,1,0:T(8,128)S(1)} %copy-done, f32[2,128,2048]{2,1,0:T(8,128)S(1)} %copy-done.1), custom_call_target="tpu_custom_call" | custom-call | tf_op jit(solution)/shard_map/pallas_call | solution.py:308
  71.5 1.0 %copy.6 = f32[128,2048]{1,0:T(8,128)} copy(f32[128,2048]{1,0:T(8,128)S(1)} %shard_map.46) | data formatting | bytes 2097152
Async XLA Ops:
  0.0 1.6 %copy-start = (s32[2,128,2048]{2,1,0:T(8,128)S(1)}, s32[2,128,2048]{2,1,0:T(8,128)}, u32[]{:S(2)}) copy-start(s32[2,128,2048]{2,1,0:T(8,128)} %offsets_ref.1) | copy-start | bytes 6291460
  1.6 1.6 %copy-start.1 = (f32[2,128,2048]{2,1,0:T(8,128)S(1)}, f32[2,128,2048]{2,1,0:T(8,128)}, u32[]{:S(2)}) copy-start(f32[2,128,2048]{2,1,0:T(8,128)} %fractions_ref.1) | copy-start | bytes 6291460
  3.2 1.2 %copy-start.2 = (f32[2048,128]{1,0:T(8,128)S(1)}, f32[2048,128]{1,0:T(8,128)}, u32[]{:S(2)}) copy-start(f32[2048,128]{1,0:T(8,128)} %fixed_ref.1) | copy-start | bytes 3145732
  4.4 1.2 %copy-start.3 = (f32[2048,128]{1,0:T(8,128)S(1)}, f32[2048,128]{1,0:T(8,128)}, u32[]{:S(2)}) copy-start(f32[2048,128]{1,0:T(8,128)} %moving_ref.1) | copy-start | bytes 3145732

commit v2 on v1

v2 whole, which is shorter than its diff:
```python
import functools

import jax
import jax.numpy as jnp
from jax import lax
from jax.experimental import pallas as pl
from jax.experimental.pallas import tpu as pltpu
from jax.sharding import PartitionSpec as P

RADIUS = 4
REACH = 3
LANES = 128
GROUP = 8
MESH = pl.DeviceIdType.MESH
KEPT_SHIFTS = tuple(shift for shift in range(-REACH, REACH + 2) if shift != 0)


def kernel(
    strips,
    near,
    fixed_ref,
    moving_ref,
    offsets_ref,
    fractions_ref,
    out_ref,
    images,
    shifted,
    sums,
    offsets_buf,
    fractions_buf,
    send_sem,
    recv_sem,
    local_sem,
):
    me = lax.axis_index("tile")
    band = out_ref.shape[0]
    last = strips - 1
    moving_at = strips + 2
    whole = band + 2 * RADIUS
    groups = band // GROUP
    chunks = groups // 2 + 1
    pair_rows = 2 * GROUP
    first_rows = pair_rows + 2 * RADIUS

    barrier = pltpu.get_barrier_semaphore()
    for step in range(1, strips):
        pl.semaphore_signal(
            barrier, inc=1, device_id={"tile": lax.rem(me + step, strips)}, device_id_type=MESH
        )
    targets = near(me)

    def send(chunk, begin, rows, target):
        for ref, base in ((fixed_ref, 0), (moving_ref, moving_at)):
            pltpu.make_async_remote_copy(
                src_ref=ref.at[pl.ds(target * band - RADIUS + begin, rows)],
                dst_ref=images.at[base + 1 + me, pl.ds(begin, rows)],
                send_sem=send_sem.at[chunk],
                recv_sem=recv_sem.at[chunk],
                device_id={"tile": target},
                device_id_type=MESH,
            ).start()

    pl.semaphore_wait(barrier, strips - 1)
    for target in targets:
        pl.when(target == 0)(
            functools.partial(send, 0, RADIUS, first_rows - RADIUS, target)
        )
        pl.when(target != 0)(functools.partial(send, 0, 0, first_rows, target))

    def send_pair(chunk, carry):
        for target in targets:
            send(chunk, chunk * pair_rows + 2 * RADIUS, pair_rows, target)
        return carry

    lax.fori_loop(1, chunks - 2, send_pair, 0)
    for target in targets:
        send(chunks - 2, whole - pair_rows, GROUP, target)
    for target in targets:
        pl.when(target == last)(
            functools.partial(send, chunks - 1, whole - GROUP, GROUP - RADIUS, target)
        )
        pl.when(target != last)(
            functools.partial(send, chunks - 1, whole - GROUP, GROUP, target)
        )

    def own_copies(source, target, rows):
        return [
            pltpu.make_async_copy(
                ref.at[pl.ds(source, rows)],
                images.at[base + 1 + me, pl.ds(target, rows)],
                local_sem.at[place],
            )
            for place, (ref, base) in enumerate(((fixed_ref, 0), (moving_ref, moving_at)))
        ]

    first_own = own_copies(0, RADIUS, whole - RADIUS)
    last_own = own_copies(last * band - RADIUS, 0, whole - RADIUS)
    inner_own = own_copies(jnp.clip(me, 1, last - 1) * band - RADIUS, 0, whole)

    def each_own(act):
        @pl.when(me == 0)
        def _():
            for copy in first_own:
                act(copy)

        @pl.when(me == last)
        def _():
            for copy in last_own:
                act(copy)

        @pl.when(jnp.logical_and(me > 0, me < last))
        def _():
            for copy in inner_own:
                act(copy)

    each_own(lambda copy: copy.start())
    offsets_copy = pltpu.make_async_copy(offsets_ref, offsets_buf, local_sem.at[2])
    fractions_copy = pltpu.make_async_copy(fractions_ref, fractions_buf, local_sem.at[3])
    offsets_copy.start()
    fractions_copy.start()

    for base in (0, moving_at):
        for side in (base, base + strips + 1):
            images[side] = jnp.zeros(images.shape[1:], jnp.float32)

        @pl.when(me == 0)
        def _():
            images[pl.ds(base + 1, strips), 0:RADIUS, :] = jnp.zeros(
                (strips, RADIUS, LANES), jnp.float32
            )

        @pl.when(me == last)
        def _():
            images[pl.ds(base + 1, strips), whole - RADIUS : whole, :] = jnp.zeros(
                (strips, RADIUS, LANES), jnp.float32
            )

    each_own(lambda copy: copy.wait())
    offsets_copy.wait()
    fractions_copy.wait()

    lane = lax.broadcasted_iota(jnp.int32, (GROUP, LANES), 1)

    def moved(shift, base, strip, rows):
        centre = images[base + strip + 1, rows, :]
        if shift > 0:
            right = images[base + strip + 2, rows, :]
            return pltpu.roll(jnp.where(lane < shift, right, centre), LANES - shift, 1)
        if shift < 0:
            left = images[base + strip, rows, :]
            return pltpu.roll(jnp.where(lane >= LANES + shift, left, centre), -shift, 1)
        return centre

    def row_sums(row):
        rows = pl.ds(row, GROUP)

        def strip_step(strip, carry):
            totals = [None] * 5
            for shift in range(-RADIUS, RADIUS + 1):
                f = moved(shift, 0, strip, rows)
                m = moved(shift, moving_at, strip, rows)
                if shift in KEPT_SHIFTS:
                    shifted[strip, KEPT_SHIFTS.index(shift), rows, :] = m
                for place, term in enumerate((f, m, f * f, m * m, f * m)):
                    totals[place] = term if shift == -RADIUS else totals[place] + term
            for place, total in enumerate(totals):
                sums[strip, place, rows, :] = total
            return carry

        lax.fori_loop(0, strips, strip_step, 0, unroll=8)

    window_count = float((2 * RADIUS + 1) ** 2)

    def confidence(strip, row):
        windows = []
        for place in range(5):
            total = sums[strip, place, pl.ds(row, GROUP), :]
            for step in range(1, 2 * RADIUS + 1):
                total = total + sums[strip, place, pl.ds(row + step, GROUP), :]
            windows.append(total)
        fixed_sum, moving_sum, fixed_square, moving_square, cross_sum = windows
        fixed_var = fixed_square - fixed_sum * fixed_sum * (1.0 / window_count)
        moving_var = moving_square - moving_sum * moving_sum * (1.0 / window_count)
        covariance = cross_sum - fixed_sum * moving_sum * (1.0 / window_count)
        correlation = covariance * lax.rsqrt(fixed_var * moving_var + 0.001)
        return 0.5 * (1.0 + correlation)

    def pick(values, index):
        for bit in (4, 2, 1):
            chosen = jnp.bitwise_and(index, bit) != 0
            values = [
                jnp.where(chosen, values[place + bit], values[place])
                if place + bit < len(values)
                else values[place]
                for place in range(bit + 1)
            ]
        return values

    def warp(row):
        def strip_step(strip, carry):
            here = (pl.ds(row, GROUP), pl.ds(pl.multiple_of(strip * LANES, LANES), LANES))
            row_index = offsets_buf[(0,) + here] + REACH
            column_index = offsets_buf[(1,) + here] + REACH
            weight = confidence(strip, row)
            row_weight = weight * fractions_buf[(0,) + here]
            column_weight = weight * fractions_buf[(1,) + here]
            other_weight = 1.0 - column_weight
            blended = []
            for row_shift in range(-REACH, REACH + 2):
                rows = pl.ds(row + RADIUS + row_shift, GROUP)
                columns = [
                    shifted[strip, KEPT_SHIFTS.index(shift), rows, :]
                    if shift in KEPT_SHIFTS
                    else images[moving_at + 1 + strip, rows, :]
                    for shift in range(-REACH, REACH + 2)
                ]
                left, right = pick(columns, column_index)
                blended.append(other_weight * left + column_weight * right)
            upper, lower = pick(blended, row_index)
            out_ref[here] = (1.0 - row_weight) * upper + row_weight * lower
            return carry

        lax.fori_loop(0, strips, strip_step, 0)

    def count(sem, blocks, rows):
        piece = images.at[pl.ds(0, blocks), pl.ds(0, rows)]
        pltpu.make_async_copy(piece, piece, sem).wait()

    blocks = 2 * (strips - 1)

    def group_step(group, carry):
        row = pl.multiple_of(group * GROUP, GROUP)

        @pl.when(group == 0)
        def _():
            pl.when(me == 0)(
                functools.partial(count, recv_sem.at[0], blocks, first_rows - RADIUS)
            )
            pl.when(me != 0)(functools.partial(count, recv_sem.at[0], blocks, first_rows))
            row_sums(0)

        @pl.when(
            jnp.logical_and(
                jnp.logical_and(group > 0, group < groups - 2), lax.rem(group, 2) == 0
            )
        )
        def _():
            count(recv_sem.at[group // 2], blocks, pair_rows)

        @pl.when(group == groups - 2)
        def _():
            count(recv_sem.at[chunks - 2], blocks, GROUP)

        @pl.when(group == groups - 1)
        def _():
            pl.when(me == last)(
                functools.partial(count, recv_sem.at[chunks - 1], blocks, GROUP - RADIUS)
            )
            pl.when(me != last)(
                functools.partial(count, recv_sem.at[chunks - 1], blocks, GROUP)
            )

        row_sums(row + GROUP)
        warp(row)
        return carry

    lax.fori_loop(0, groups, group_step, 0)

    def sent(chunk, rows, edge):
        @pl.when(me != edge)
        def _():
            count(send_sem.at[chunk], blocks - 2, rows)
            count(send_sem.at[chunk], 2, rows - RADIUS)

        pl.when(me == edge)(functools.partial(count, send_sem.at[chunk], blocks, rows))

    sent(0, first_rows, 0)
    for chunk in range(1, chunks - 2):
        count(send_sem.at[chunk], blocks, pair_rows)
    count(send_sem.at[chunks - 2], blocks, GROUP)
    sent(chunks - 1, GROUP, last)


def solution(mesh):
    strips = mesh.shape["tile"]
    ring = 8

    def near(me):
        z, y = lax.rem(me, ring), me // ring
        steps = [(0, 1)]
        for far in range(1, ring // 2 + 1):
            for sign in (1, -1) if far < ring // 2 else (1,):
                steps += [(sign * far, 0), (sign * far, 1)]
        return [
            lax.rem(z + dz + ring, ring) + ring * lax.rem(y + dy, strips // ring)
            for dz, dy in steps
        ]

    def on_device(fixed, moving, offsets, fractions):
        band, width = offsets.shape[1:]
        padded = band + 2 * RADIUS + 2 * GROUP
        chunks = band // GROUP // 2 + 1
        return pl.pallas_call(
            functools.partial(kernel, strips, near),
            out_shape=jax.ShapeDtypeStruct((band, width), jnp.float32),
            in_specs=[pl.BlockSpec(memory_space=pl.ANY)] * 4,
            out_specs=pl.BlockSpec(memory_space=pltpu.VMEM),
            scratch_shapes=[
                pltpu.VMEM((2 * (strips + 2), padded, LANES), jnp.float32),
                pltpu.VMEM((strips, len(KEPT_SHIFTS), padded, LANES), jnp.float32),
                pltpu.VMEM((strips, 5, padded, LANES), jnp.float32),
                pltpu.VMEM(offsets.shape, offsets.dtype),
                pltpu.VMEM(fractions.shape, fractions.dtype),
                pltpu.SemaphoreType.DMA((chunks,)),
                pltpu.SemaphoreType.DMA((chunks,)),
                pltpu.SemaphoreType.DMA((4,)),
            ],
            compiler_params=pltpu.CompilerParams(
                collective_id=0, has_side_effects=True, vmem_limit_bytes=63 * 2**20
            ),
        )(fixed, moving, offsets, fractions)

    placed = (
        P("pair", "tile"),
        P("pair", "tile"),
        P(None, ("pair", "tile"), None),
        P(None, ("pair", "tile"), None),
    )
    return jax.shard_map(
        on_device, mesh=mesh, in_specs=placed, out_specs=P(("pair", "tile"), None), check_vma=False
    )
```

time: 72.7 us -> 62.5 us (0.86)
  Pallas kernels: 65.9 us -> 60.1 us
  local copies, waits for them, and re-layouts: 6.6 us -> 2.3 us
    pallas_call x1, Pallas kernels: 65.9 us -> 60.1 us  [on_device(): pl.pallas_call(functools.partial(kernel, strips, near), out_shape=jax.Sha...]
    unnamed x9 -> x1, local copies, waits for them, and re-layouts: 6.6 us -> 2.3 us
where the time goes in v2:
time: 62.5 us; the launch traced here: 62.4 us
  Pallas kernels  60.1 us (96%)
  local copies, waits for them, and re-layouts  2.3 us (4%)
    pallas_call x1, Pallas kernels, on_device(): pl.pallas_call(functools.partial(kernel, strips, near), out_shape=jax.Sha...  60.1 us
    unnamed x1, local copies, waits for them, and re-layouts  2.3 us

profile of v2, /device:TPU:36, one launch (start us, length us, event | category | flops | bytes accessed | tf_op | source)
XLA Modules:
  0.0 62.4 jit_solution(9156592791867706422)
XLA Ops:
  0.0 60.1 %shard_map.46 = f32[128,2048]{1,0:T(8,128)} custom-call(f32[2048,128]{1,0:T(8,128)} %fixed_ref.1, f32[2048,128]{1,0:T(8,128)} %moving_ref.1, s32[2,128,2048]{2,1,0:T(8,128)} %offsets_ref.1, f32[2,128,2048]{2,1,0:T(8,128)} %fractions_ref.1), custom_call_target="tpu_custom_call" | custom-call | tf_op jit(solution)/shard_map/pallas_call | solution.py:303
  60.1 2.3 %copy.6 = f32[128,2048]{1,0:T(8,128)} copy(f32[128,2048]{1,0:T(8,128)} %shard_map.46) | data formatting | bytes 2097152

commit v3 on v2

--- a/solution.py
+++ b/solution.py
@@ -11,13 +11,13 @@
 REACH = 3
 LANES = 128
 GROUP = 8
+CHUNKS = (4, 4, 4, 2, 1, 1)
 MESH = pl.DeviceIdType.MESH
 KEPT_SHIFTS = tuple(shift for shift in range(-REACH, REACH + 2) if shift != 0)
 
 
 def kernel(
     strips,
-    near,
     fixed_ref,
     moving_ref,
     offsets_ref,
@@ -31,57 +31,84 @@
     send_sem,
     recv_sem,
     local_sem,
+    ready_sem,
 ):
     me = lax.axis_index("tile")
     band = out_ref.shape[0]
     last = strips - 1
     moving_at = strips + 2
     whole = band + 2 * RADIUS
-    groups = band // GROUP
-    chunks = groups // 2 + 1
-    pair_rows = 2 * GROUP
-    first_rows = pair_rows + 2 * RADIUS
+    blocks = 2 * last
+    chunks = len(CHUNKS)
+    begins = [0] + [2 * RADIUS + GROUP * sum(CHUNKS[: chunk + 1]) for chunk in range(chunks)]
+
+    def send(chunk, target):
+        def rows_of(begin, end):
+            for ref, base in ((fixed_ref, 0), (moving_ref, moving_at)):
+                pltpu.make_async_remote_copy(
+                    src_ref=ref.at[pl.ds(target * band - RADIUS + begin, end - begin)],
+                    dst_ref=images.at[base + 1 + me, pl.ds(begin, end - begin)],
+                    send_sem=send_sem.at[chunk],
+                    recv_sem=recv_sem.at[chunk],
+                    device_id={"tile": target},
+                    device_id_type=MESH,
+                ).start()
+
+        begin, end = begins[chunk], begins[chunk + 1]
+        if chunk == 0:
+            pl.when(target == 0)(lambda: rows_of(begin + RADIUS, end))
+            pl.when(target != 0)(lambda: rows_of(begin, end))
+        elif chunk == chunks - 1:
+            pl.when(target == last)(lambda: rows_of(begin, end - RADIUS))
+            pl.when(target != last)(lambda: rows_of(begin, end))
+        else:
+            rows_of(begin, end)
+
+    ring = strips // 2
+    here_z, here_y = lax.rem(me, ring), me // ring
+
+    def target_at(place):
+        apart = place + 3
+        distance = apart // 4
+        way = 1 - 2 * (lax.rem(apart, 4) // 2)
+        z = lax.rem(here_z + distance * way + ring, ring)
+        return z + ring * lax.rem(here_y + lax.rem(apart, 2), 2)
+
+    def send_range(chunk, low, high, backward=False):
+        def step(index, carry):
+            send(chunk, target_at(high - 1 - index if backward else low + index))
+            return carry
+
+        lax.fori_loop(0, high - low, step, 0)
 
     barrier = pltpu.get_barrier_semaphore()
-    for step in range(1, strips):
+    for place in range(5):
         pl.semaphore_signal(
-            barrier, inc=1, device_id={"tile": lax.rem(me + step, strips)}, device_id_type=MESH
+            barrier, inc=1, device_id={"tile": target_at(jnp.int32(place))}, device_id_type=MESH
         )
-    targets = near(me)
-
-    def send(chunk, begin, rows, target):
-        for ref, base in ((fixed_ref, 0), (moving_ref, moving_at)):
-            pltpu.make_async_remote_copy(
-                src_ref=ref.at[pl.ds(target * band - RADIUS + begin, rows)],
-                dst_ref=images.at[base + 1 + me, pl.ds(begin, rows)],
-                send_sem=send_sem.at[chunk],
-                recv_sem=recv_sem.at[chunk],
-                device_id={"tile": target},
+    pl.semaphore_wait(barrier, 5)
+
+    def tell_beside(phase):
+        for place in (1, 3):
+            pl.semaphore_signal(
+                ready_sem.at[phase],
+                inc=1,
+                device_id={"tile": target_at(jnp.int32(place))},
                 device_id_type=MESH,
-            ).start()
-
-    pl.semaphore_wait(barrier, strips - 1)
-    for target in targets:
-        pl.when(target == 0)(
-            functools.partial(send, 0, RADIUS, first_rows - RADIUS, target)
-        )
-        pl.when(target != 0)(functools.partial(send, 0, 0, first_rows, target))
-
-    def send_pair(chunk, carry):
-        for target in targets:
-            send(chunk, chunk * pair_rows + 2 * RADIUS, pair_rows, target)
-        return carry
-
-    lax.fori_loop(1, chunks - 2, send_pair, 0)
-    for target in targets:
-        send(chunks - 2, whole - pair_rows, GROUP, target)
-    for target in targets:
-        pl.when(target == last)(
-            functools.partial(send, chunks - 1, whole - GROUP, GROUP - RADIUS, target)
-        )
-        pl.when(target != last)(
-            functools.partial(send, chunks - 1, whole - GROUP, GROUP, target)
-        )
+            )
+
+    ends = (5, 9, 13, 15)
+    tell_beside(0)
+    send_range(0, 0, 5)
+    send_range(1, 0, 5)
+    for phase in range(3):
+        pl.semaphore_wait(ready_sem.at[phase], 2)
+        if phase < 2:
+            tell_beside(phase + 1)
+        send_range(0, ends[phase], ends[phase + 1])
+    send_range(1, 5, last)
+    for chunk in range(2, chunks):
+        send_range(chunk, 0, last, backward=chunk == chunks - 1)
 
     def own_copies(source, target, rows):
         return [
@@ -167,7 +194,7 @@
                 sums[strip, place, rows, :] = total
             return carry
 
-        lax.fori_loop(0, strips, strip_step, 0, unroll=8)
+        lax.fori_loop(0, strips, strip_step, 0, unroll=strips)
 
     window_count = float((2 * RADIUS + 1) ** 2)
 
@@ -226,84 +253,60 @@
         piece = images.at[pl.ds(0, blocks), pl.ds(0, rows)]
         pltpu.make_async_copy(piece, piece, sem).wait()
 
-    blocks = 2 * (strips - 1)
+    def arrived(chunk):
+        rows = begins[chunk + 1] - begins[chunk]
+        full = functools.partial(count, recv_sem.at[chunk], blocks, rows)
+        if chunk in (0, chunks - 1):
+            pl.when(me == (last if chunk else 0))(
+                functools.partial(count, recv_sem.at[chunk], blocks, rows - RADIUS)
+            )
+            pl.when(me != (last if chunk else 0))(full)
+        else:
+            full()
+
+    def sent(chunk):
+        rows = begins[chunk + 1] - begins[chunk]
+        full = functools.partial(count, send_sem.at[chunk], blocks, rows)
+        if chunk in (0, chunks - 1):
+            pl.when(me == (last if chunk else 0))(full)
+
+            @pl.when(me != (last if chunk else 0))
+            def _():
+                count(send_sem.at[chunk], blocks - 2, rows)
+                count(send_sem.at[chunk], 2, rows - RADIUS)
+        else:
+            full()
 
     def group_step(group, carry):
         row = pl.multiple_of(group * GROUP, GROUP)
-
-        @pl.when(group == 0)
-        def _():
-            pl.when(me == 0)(
-                functools.partial(count, recv_sem.at[0], blocks, first_rows - RADIUS)
-            )
-            pl.when(me != 0)(functools.partial(count, recv_sem.at[0], blocks, first_rows))
-            row_sums(0)
-
-        @pl.when(
-            jnp.logical_and(
-                jnp.logical_and(group > 0, group < groups - 2), lax.rem(group, 2) == 0
-            )
-        )
-        def _():
-            count(recv_sem.at[group // 2], blocks, pair_rows)
-
-        @pl.when(group == groups - 2)
-        def _():
-            count(recv_sem.at[chunks - 2], blocks, GROUP)
-
-        @pl.when(group == groups - 1)
-        def _():
-            pl.when(me == last)(
-                functools.partial(count, recv_sem.at[chunks - 1], blocks, GROUP - RADIUS)
-            )
-            pl.when(me != last)(
-                functools.partial(count, recv_sem.at[chunks - 1], blocks, GROUP)
-            )
+        for chunk in range(chunks):
+
+            @pl.when(group == sum(CHUNKS[:chunk]))
+            def _():
+                arrived(chunk)
+                if chunk == 0:
+                    row_sums(0)
 
         row_sums(row + GROUP)
         warp(row)
         return carry
 
-    lax.fori_loop(0, groups, group_step, 0)
-
-    def sent(chunk, rows, edge):
-        @pl.when(me != edge)
-        def _():
-            count(send_sem.at[chunk], blocks - 2, rows)
-            count(send_sem.at[chunk], 2, rows - RADIUS)
-
-        pl.when(me == edge)(functools.partial(count, send_sem.at[chunk], blocks, rows))
-
-    sent(0, first_rows, 0)
-    for chunk in range(1, chunks - 2):
-        count(send_sem.at[chunk], blocks, pair_rows)
-    count(send_sem.at[chunks - 2], blocks, GROUP)
-    sent(chunks - 1, GROUP, last)
+    lax.fori_loop(0, band // GROUP, group_step, 0)
+    for chunk in range(chunks):
+        sent(chunk)
 
 
 def solution(mesh):
     strips = mesh.shape["tile"]
-    ring = 8
-
-    def near(me):
-        z, y = lax.rem(me, ring), me // ring
-        steps = [(0, 1)]
-        for far in range(1, ring // 2 + 1):
-            for sign in (1, -1) if far < ring // 2 else (1,):
-                steps += [(sign * far, 0), (sign * far, 1)]
-        return [
-            lax.rem(z + dz + ring, ring) + ring * lax.rem(y + dy, strips // ring)
-            for dz, dy in steps
-        ]
 
     def on_device(fixed, moving, offsets, fractions):
         band, width = offsets.shape[1:]
         padded = band + 2 * RADIUS + 2 * GROUP
-        chunks = band // GROUP // 2 + 1
+        chunks = len(CHUNKS)
         return pl.pallas_call(
-            functools.partial(kernel, strips, near),
-            out_shape=jax.ShapeDtypeStruct((band, width), jnp.float32),
-            in_specs=[pl.BlockSpec(memory_space=pl.ANY)] * 4,
+            functools.partial(kernel, strips),
+            out_shape=pltpu.VMEM((band, width), jnp.float32),
+            in_specs=[pl.BlockSpec(memory_space=pltpu.HBM)] * 4,
             out_specs=pl.BlockSpec(memory_space=pltpu.VMEM),
             scratch_shapes=[
                 pltpu.VMEM((2 * (strips + 2), padded, LANES), jnp.float32),
@@ -314,9 +317,10 @@
                 pltpu.SemaphoreType.DMA((chunks,)),
                 pltpu.SemaphoreType.DMA((chunks,)),
                 pltpu.SemaphoreType.DMA((4,)),
+                pltpu.SemaphoreType.REGULAR((3,)),
             ],
             compiler_params=pltpu.CompilerParams(
-                collective_id=0, has_side_effects=True, vmem_limit_bytes=63 * 2**20
+                collective_id=0, has_side_effects=True, vmem_limit_bytes=60 * 2**20
             ),
         )(fixed, moving, offsets, fractions)
 

time: 62.5 us -> 59.2 us (0.947)
  Pallas kernels: 60.1 us -> 58.1 us
  local copies, waits for them, and re-layouts: 2.3 us -> 0.97 us
    pallas_call x1, Pallas kernels: 60.1 us -> 58.1 us  [on_device(): pl.pallas_call(functools.partial(kernel, strips), out_shape=pltpu.VMEM((b...]
    unnamed x1, local copies, waits for them, and re-layouts: 2.3 us -> 0.97 us
where the time goes in v3:
time: 59.2 us; the launch traced here: 59.1 us
  Pallas kernels  58.1 us (98%)
  local copies, waits for them, and re-layouts  0.97 us (2%)
    pallas_call x1, Pallas kernels, on_device(): pl.pallas_call(functools.partial(kernel, strips), out_shape=pltpu.VMEM((b...  58.1 us

profile of v3, /device:TPU:36, one launch (start us, length us, event | category | flops | bytes accessed | tf_op | source)
XLA Modules:
  0.0 59.1 jit_solution(3153070156884913498)
XLA Ops:
  0.0 58.1 %shard_map.46 = f32[128,2048]{1,0:T(8,128)S(1)} custom-call(f32[2048,128]{1,0:T(8,128)} %fixed_ref.1, f32[2048,128]{1,0:T(8,128)} %moving_ref.1, s32[2,128,2048]{2,1,0:T(8,128)} %offsets_ref.1, f32[2,128,2048]{2,1,0:T(8,128)} %fractions_ref.1), custom_call_target="tpu_custom_call" | custom-call | tf_op jit(solution)/shard_map/pallas_call | solution.py:306
  58.1 1.0 %copy.6 = f32[128,2048]{1,0:T(8,128)} copy(f32[128,2048]{1,0:T(8,128)S(1)} %shard_map.46) | data formatting | bytes 2097152

commit v4 on v3

--- a/solution.py
+++ b/solution.py
@@ -26,6 +26,7 @@
     images,
     shifted,
     sums,
+    triples,
     offsets_buf,
     fractions_buf,
     send_sem,
@@ -108,7 +109,7 @@
         send_range(0, ends[phase], ends[phase + 1])
     send_range(1, 5, last)
     for chunk in range(2, chunks):
-        send_range(chunk, 0, last, backward=chunk == chunks - 1)
+        send_range(chunk, 0, last, backward=True)
 
     def own_copies(source, target, rows):
         return [
@@ -161,6 +162,8 @@
             images[pl.ds(base + 1, strips), whole - RADIUS : whole, :] = jnp.zeros(
                 (strips, RADIUS, LANES), jnp.float32
             )
+
+    sums[:, :, 0:GROUP, :] = jnp.zeros((strips, 5, GROUP, LANES), jnp.float32)
 
     each_own(lambda copy: copy.wait())
     offsets_copy.wait()
@@ -178,32 +181,35 @@
             return pltpu.roll(jnp.where(lane >= LANES + shift, left, centre), -shift, 1)
         return centre
 
-    def row_sums(row):
+    def both_moved(strip, row):
+        return [
+            [moved(shift, base, strip, pl.ds(row, GROUP)) for base in (0, moving_at)]
+            for shift in range(-RADIUS, RADIUS + 1)
+        ]
+
+    def row_sums(strip, row, images_moved):
         rows = pl.ds(row, GROUP)
-
-        def strip_step(strip, carry):
-            totals = [None] * 5
-            for shift in range(-RADIUS, RADIUS + 1):
-                f = moved(shift, 0, strip, rows)
-                m = moved(shift, moving_at, strip, rows)
-                if shift in KEPT_SHIFTS:
-                    shifted[strip, KEPT_SHIFTS.index(shift), rows, :] = m
-                for place, term in enumerate((f, m, f * f, m * m, f * m)):
-                    totals[place] = term if shift == -RADIUS else totals[place] + term
-            for place, total in enumerate(totals):
-                sums[strip, place, rows, :] = total
-            return carry
-
-        lax.fori_loop(0, strips, strip_step, 0, unroll=strips)
+        totals = [None] * 5
+        for shift, (f, m) in zip(range(-RADIUS, RADIUS + 1), images_moved):
+            if shift in KEPT_SHIFTS:
+                shifted[strip, KEPT_SHIFTS.index(shift), rows, :] = m
+            for place, term in enumerate((f, m, f * f, m * m, f * m)):
+                totals[place] = term if shift == -RADIUS else totals[place] + term
+        for place, total in enumerate(totals):
+            sums[strip, place, pl.ds(row + GROUP, GROUP), :] = total
+            triples[strip, place, pl.ds(row + GROUP - 2, GROUP), :] = total + (
+                sums[strip, place, pl.ds(row + GROUP - 1, GROUP), :]
+                + sums[strip, place, pl.ds(row + GROUP - 2, GROUP), :]
+            )
 
     window_count = float((2 * RADIUS + 1) ** 2)
 
     def confidence(strip, row):
         windows = []
         for place in range(5):
-            total = sums[strip, place, pl.ds(row, GROUP), :]
-            for step in range(1, 2 * RADIUS + 1):
-                total = total + sums[strip, place, pl.ds(row + step, GROUP), :]
+            total = triples[strip, place, pl.ds(row + GROUP, GROUP), :]
+            for step in (3, 6):
+                total = total + triples[strip, place, pl.ds(row + GROUP + step, GROUP), :]
             windows.append(total)
         fixed_sum, moving_sum, fixed_square, moving_square, cross_sum = windows
         fixed_var = fixed_square - fixed_sum * fixed_sum * (1.0 / window_count)
@@ -223,31 +229,27 @@
             ]
         return values
 
-    def warp(row):
-        def strip_step(strip, carry):
-            here = (pl.ds(row, GROUP), pl.ds(pl.multiple_of(strip * LANES, LANES), LANES))
-            row_index = offsets_buf[(0,) + here] + REACH
-            column_index = offsets_buf[(1,) + here] + REACH
-            weight = confidence(strip, row)
-            row_weight = weight * fractions_buf[(0,) + here]
-            column_weight = weight * fractions_buf[(1,) + here]
-            other_weight = 1.0 - column_weight
-            blended = []
-            for row_shift in range(-REACH, REACH + 2):
-                rows = pl.ds(row + RADIUS + row_shift, GROUP)
-                columns = [
-                    shifted[strip, KEPT_SHIFTS.index(shift), rows, :]
-                    if shift in KEPT_SHIFTS
-                    else images[moving_at + 1 + strip, rows, :]
-                    for shift in range(-REACH, REACH + 2)
-                ]
-                left, right = pick(columns, column_index)
-                blended.append(other_weight * left + column_weight * right)
-            upper, lower = pick(blended, row_index)
-            out_ref[here] = (1.0 - row_weight) * upper + row_weight * lower
-            return carry
-
-        lax.fori_loop(0, strips, strip_step, 0)
+    def warp(strip, row):
+        here = (pl.ds(row, GROUP), pl.ds(pl.multiple_of(strip * LANES, LANES), LANES))
+        row_index = offsets_buf[(0,) + here] + REACH
+        column_index = offsets_buf[(1,) + here] + REACH
+        weight = confidence(strip, row)
+        row_weight = weight * fractions_buf[(0,) + here]
+        column_weight = weight * fractions_buf[(1,) + here]
+        other_weight = 1.0 - column_weight
+        blended = []
+        for row_shift in range(-REACH, REACH + 2):
+            rows = pl.ds(row + RADIUS + row_shift, GROUP)
+            columns = [
+                shifted[strip, KEPT_SHIFTS.index(shift), rows, :]
+                if shift in KEPT_SHIFTS
+                else images[moving_at + 1 + strip, rows, :]
+                for shift in range(-REACH, REACH + 2)
+            ]
+            left, right = pick(columns, column_index)
+            blended.append(other_weight * left + column_weight * right)
+        upper, lower = pick(blended, row_index)
+        out_ref[here] = (1.0 - row_weight) * upper + row_weight * lower
 
     def count(sem, blocks, rows):
         piece = images.at[pl.ds(0, blocks), pl.ds(0, rows)]
@@ -285,10 +287,23 @@
             def _():
                 arrived(chunk)
                 if chunk == 0:
-                    row_sums(0)
-
-        row_sums(row + GROUP)
-        warp(row)
+
+                    def first_step(strip, carry):
+                        row_sums(strip, 0, both_moved(strip, 0))
+                        return carry
+
+                    lax.fori_loop(0, strips, first_step, 0, unroll=4)
+
+        def sums_step(strip, carry):
+            row_sums(strip, row + GROUP, both_moved(strip, row + GROUP))
+            return carry
+
+        def warp_step(strip, carry):
+            warp(strip, row)
+            return carry
+
+        lax.fori_loop(0, strips, sums_step, 0, unroll=16)
+        lax.fori_loop(0, strips, warp_step, 0, unroll=4)
         return carry
 
     lax.fori_loop(0, band // GROUP, group_step, 0)
@@ -312,6 +327,7 @@
                 pltpu.VMEM((2 * (strips + 2), padded, LANES), jnp.float32),
                 pltpu.VMEM((strips, len(KEPT_SHIFTS), padded, LANES), jnp.float32),
                 pltpu.VMEM((strips, 5, padded, LANES), jnp.float32),
+                pltpu.VMEM((strips, 5, padded, LANES), jnp.float32),
                 pltpu.VMEM(offsets.shape, offsets.dtype),
                 pltpu.VMEM(fractions.shape, fractions.dtype),
                 pltpu.SemaphoreType.DMA((chunks,)),

time: 59.2 us -> 57.9 us (0.978)
  Pallas kernels: 58.1 us -> 56.7 us
    pallas_call x1, Pallas kernels: 58.1 us -> 56.7 us  [on_device(): pl.pallas_call(functools.partial(kernel, strips), out_shape=pltpu.VMEM((b...]
where the time goes in v4:
time: 57.9 us; the launch traced here: 57.7 us
  Pallas kernels  56.7 us (98%)
  local copies, waits for them, and re-layouts  0.97 us (2%)
    pallas_call x1, Pallas kernels, on_device(): pl.pallas_call(functools.partial(kernel, strips), out_shape=pltpu.VMEM((b...  56.7 us

profile of v4, /device:TPU:36, one launch (start us, length us, event | category | flops | bytes accessed | tf_op | source)
XLA Modules:
  0.0 57.7 jit_solution(4238619555220259214)
XLA Ops:
  0.0 56.7 %shard_map.46 = f32[128,2048]{1,0:T(8,128)S(1)} custom-call(f32[2048,128]{1,0:T(8,128)} %fixed_ref.1, f32[2048,128]{1,0:T(8,128)} %moving_ref.1, s32[2,128,2048]{2,1,0:T(8,128)} %offsets_ref.1, f32[2,128,2048]{2,1,0:T(8,128)} %fractions_ref.1), custom_call_target="tpu_custom_call" | custom-call | tf_op jit(solution)/shard_map/pallas_call | solution.py:321
  56.7 1.0 %copy.6 = f32[128,2048]{1,0:T(8,128)} copy(f32[128,2048]{1,0:T(8,128)S(1)} %shard_map.46) | data formatting | bytes 2097152

commit v5 on v4

v5 whole, which is shorter than its diff:
```python
import functools

import jax
import jax.numpy as jnp
from jax import lax
from jax.experimental import pallas as pl
from jax.experimental.pallas import tpu as pltpu
from jax.sharding import PartitionSpec as P

RADIUS = 4
REACH = 3
LANES = 128
GROUP = 8
CHUNKS = (4, 4, 4, 1, 1, 1)
MESH = pl.DeviceIdType.MESH
KEPT_SHIFTS = (-3, -2, -1, 1, 2, 3, 4, -4)


def kernel(
    strips,
    fixed_ref,
    moving_ref,
    offsets_ref,
    fractions_ref,
    out_ref,
    images,
    shifted,
    sums,
    triples,
    offsets_buf,
    fractions_buf,
    send_sem,
    recv_sem,
    local_sem,
    ready_sem,
    edge_send_sem,
    edge_recv_sem,
    corner_buf,
):
    me = lax.axis_index("tile")
    band = out_ref.shape[0]
    last = strips - 1
    moving_at = strips + 2
    whole = band + 2 * RADIUS
    blocks = 2 * last
    chunks = len(CHUNKS)
    begins = [RADIUS] + [2 * RADIUS + GROUP * sum(CHUNKS[: chunk + 1]) for chunk in range(chunks)]

    both_images = ((fixed_ref, 0), (moving_ref, moving_at))

    def send(chunk, target, sent_images, place):
        def rows_of(begin, end):
            for ref, base in sent_images:
                pltpu.make_async_remote_copy(
                    src_ref=ref.at[pl.ds(target * band - RADIUS + begin, end - begin)],
                    dst_ref=images.at[base + 1 + me, pl.ds(begin, end - begin)],
                    send_sem=send_sem.at[place],
                    recv_sem=recv_sem.at[place],
                    device_id={"tile": target},
                    device_id_type=MESH,
                ).start()

        rows_of(begins[chunk], begins[chunk + 1])
        if chunk == 0:
            rows_of(begins[-1], whole - RADIUS)

    ring = strips // 2
    here_z, here_y = lax.rem(me, ring), me // ring

    def target_at(place):
        apart = place + 3
        distance = apart // 4
        way = 1 - 2 * (lax.rem(apart, 4) // 2)
        z = lax.rem(here_z + distance * way + ring, ring)
        return z + ring * lax.rem(here_y + lax.rem(apart, 2), 2)

    def send_range(chunk, low, high, backward=False, sent_images=both_images, place=None):
        def step(index, carry):
            target = target_at(high - 1 - index if backward else low + index)
            send(chunk, target, sent_images, chunk if place is None else place)
            return carry

        lax.fori_loop(0, high - low, step, 0)

    barrier = pltpu.get_barrier_semaphore()
    for place in range(5):
        pl.semaphore_signal(
            barrier, inc=1, device_id={"tile": target_at(jnp.int32(place))}, device_id_type=MESH
        )
    pl.semaphore_wait(barrier, 5)

    def tell_beside(phase):
        for place in (1, 3):
            pl.semaphore_signal(
                ready_sem.at[phase],
                inc=1,
                device_id={"tile": target_at(jnp.int32(place))},
                device_id_type=MESH,
            )

    ends = (5, 9, 13, 15)
    tell_beside(0)
    send_range(0, 0, 5)
    send_range(1, 0, 5)
    for phase in range(3):
        pl.semaphore_wait(ready_sem.at[phase], 2)
        if phase < 2:
            tell_beside(phase + 1)
        send_range(0, ends[phase], ends[phase + 1])
    send_range(1, 5, last)

    own_copies = [
        pltpu.make_async_copy(
            ref.at[pl.ds(me * band, band)],
            images.at[base + 1 + me, pl.ds(RADIUS, band)],
            local_sem.at[place],
        )
        for place, (ref, base) in enumerate(((fixed_ref, 0), (moving_ref, moving_at)))
    ]
    for copy in own_copies:
        copy.start()
    offsets_copy = pltpu.make_async_copy(offsets_ref, offsets_buf, local_sem.at[2])
    fractions_copy = pltpu.make_async_copy(fractions_ref, fractions_buf, local_sem.at[3])
    offsets_copy.start()
    fractions_copy.start()

    for base in (0, moving_at):
        for side in (base, base + strips + 1):
            images[side] = jnp.zeros(images.shape[1:], jnp.float32)

        @pl.when(me == 0)
        def _():
            images[pl.ds(base + 1, strips), 0:RADIUS, :] = jnp.zeros(
                (strips, RADIUS, LANES), jnp.float32
            )

        @pl.when(me == last)
        def _():
            images[pl.ds(base + 1, strips), whole - RADIUS : whole, :] = jnp.zeros(
                (strips, RADIUS, LANES), jnp.float32
            )

    sums[:, :, 0:GROUP, :] = jnp.zeros((strips, 5, GROUP, LANES), jnp.float32)

    def count(sem, blocks, rows):
        piece = images.at[pl.ds(0, blocks), pl.ds(0, rows)]
        pltpu.make_async_copy(piece, piece, sem).wait()

    def chunk_rows(chunk):
        return begins[chunk + 1] - begins[chunk] + (RADIUS if chunk == 0 else 0)

    def passed_on(beside, source, target, place):
        return [
            pltpu.make_async_remote_copy(
                src_ref=images.at[pl.ds(base + 1, strips), pl.ds(source, RADIUS)],
                dst_ref=images.at[pl.ds(base + 1, strips), pl.ds(target, RADIUS)],
                send_sem=edge_send_sem.at[place],
                recv_sem=edge_recv_sem.at[place],
                device_id={"tile": beside},
                device_id_type=MESH,
            )
            for base in (0, moving_at)
        ]

    for copy in own_copies:
        copy.wait()
    count(recv_sem.at[0], blocks, chunk_rows(0))

    @pl.when(me > 0)
    def _():
        for copy in passed_on(me - 1, RADIUS, whole - RADIUS, 0):
            copy.start()

    @pl.when(me < last)
    def _():
        for copy in passed_on(me + 1, whole - 2 * RADIUS, 0, 1):
            copy.start()

    for chunk in range(2, chunks - 1):
        send_range(chunk, 0, last, backward=True)
    send_range(chunks - 1, 0, last, True, both_images[1:], chunks - 1)
    send_range(chunks - 1, 0, last, True, both_images[:1], chunks)
    offsets_copy.wait()
    fractions_copy.wait()

    lane = lax.broadcasted_iota(jnp.int32, (GROUP, LANES), 1)

    def moved(shift, base, strip, rows):
        centre = images[base + strip + 1, rows, :]
        if shift > 0:
            right = images[base + strip + 2, rows, :]
            return pltpu.roll(jnp.where(lane < shift, right, centre), LANES - shift, 1)
        if shift < 0:
            left = images[base + strip, rows, :]
            return pltpu.roll(jnp.where(lane >= LANES + shift, left, centre), -shift, 1)
        return centre

    shifts = range(-RADIUS, RADIUS + 1)

    def image_moved(base, strip, row):
        return [moved(shift, base, strip, pl.ds(row, GROUP)) for shift in shifts]

    def moved_before(strip, row):
        rows = pl.ds(row, GROUP)
        return [
            shifted[strip, KEPT_SHIFTS.index(shift), rows, :]
            if shift
            else images[moving_at + 1 + strip, rows, :]
            for shift in shifts
        ]

    def keep(strip, row, moving_moved, kept):
        for shift, m in zip(shifts, moving_moved):
            if shift in kept:
                shifted[strip, KEPT_SHIFTS.index(shift), pl.ds(row, GROUP), :] = m

    def sums_of_three(strip, row):
        for place in range(5):
            triples[strip, place, pl.ds(row + GROUP - 2, GROUP), :] = (
                sums[strip, place, pl.ds(row + GROUP, GROUP), :]
                + sums[strip, place, pl.ds(row + GROUP - 1, GROUP), :]
                + sums[strip, place, pl.ds(row + GROUP - 2, GROUP), :]
            )

    def store_sums(strip, row, terms_of_shifts):
        totals = {}
        for terms in terms_of_shifts:
            for place, term in terms.items():
                totals[place] = totals[place] + term if place in totals else term
        for place, total in totals.items():
            sums[strip, place, pl.ds(row + GROUP, GROUP), :] = total

    def row_sums(strip, row):
        fixed_moved = image_moved(0, strip, row)
        moving_moved = image_moved(moving_at, strip, row)
        keep(strip, row, moving_moved, KEPT_SHIFTS[:-1])
        store_sums(
            strip,
            row,
            [
                {0: f, 1: m, 2: f * f, 3: m * m, 4: f * m}
                for f, m in zip(fixed_moved, moving_moved)
            ],
        )

    def row_sums_of_moving(strip, row):
        moving_moved = image_moved(moving_at, strip, row)
        keep(strip, row, moving_moved, KEPT_SHIFTS)
        store_sums(strip, row, [{1: m, 3: m * m} for m in moving_moved])

    def row_sums_with_fixed(strip, row):
        pairs = zip(image_moved(0, strip, row), moved_before(strip, row))
        store_sums(strip, row, [{0: f, 2: f * f, 4: f * m} for f, m in pairs])

    window_count = float((2 * RADIUS + 1) ** 2)

    def confidence(strip, row):
        windows = []
        for place in range(5):
            total = triples[strip, place, pl.ds(row + GROUP, GROUP), :]
            for step in (3, 6):
                total = total + triples[strip, place, pl.ds(row + GROUP + step, GROUP), :]
            windows.append(total)
        fixed_sum, moving_sum, fixed_square, moving_square, cross_sum = windows
        fixed_var = fixed_square - fixed_sum * fixed_sum * (1.0 / window_count)
        moving_var = moving_square - moving_sum * moving_sum * (1.0 / window_count)
        covariance = cross_sum - fixed_sum * moving_sum * (1.0 / window_count)
        correlation = covariance * lax.rsqrt(fixed_var * moving_var + 0.001)
        return 0.5 * (1.0 + correlation)

    def pick(values, index):
        for bit in (4, 2, 1):
            chosen = jnp.bitwise_and(index, bit) != 0
            values = [
                jnp.where(chosen, values[place + bit], values[place])
                if place + bit < len(values)
                else values[place]
                for place in range(bit + 1)
            ]
        return values

    def band_place(strip, row):
        return pl.ds(row, GROUP), pl.ds(pl.multiple_of(strip * LANES, LANES), LANES)

    def corners(strip, row):
        here = band_place(strip, row)
        column_index = offsets_buf[(1,) + here] + REACH
        row_index = offsets_buf[(0,) + here] + REACH
        lefts, rights = [], []
        for row_shift in range(-REACH, REACH + 2):
            columns = moved_before(strip, row + RADIUS + row_shift)
            left, right = pick(columns[RADIUS - REACH :], column_index)
            lefts.append(left)
            rights.append(right)
        return pick(lefts, row_index) + pick(rights, row_index)

    def blend(strip, row, top_left, bottom_left, top_right, bottom_right):
        here = band_place(strip, row)
        weight = confidence(strip, row)
        row_weight = weight * fractions_buf[(0,) + here]
        column_weight = weight * fractions_buf[(1,) + here]
        upper = (1.0 - column_weight) * top_left + column_weight * top_right
        lower = (1.0 - column_weight) * bottom_left + column_weight * bottom_right
        out_ref[here] = (1.0 - row_weight) * upper + row_weight * lower

    def group_step(group, carry):
        row = pl.multiple_of(group * GROUP, GROUP)
        for chunk in range(1, chunks - 1):
            pl.when(group == sum(CHUNKS[:chunk]))(
                functools.partial(count, recv_sem.at[chunk], blocks, chunk_rows(chunk))
            )

        def sums_step(strip, carry):
            row_sums(strip, row + GROUP)
            sums_of_three(strip, row + GROUP)
            return carry

        def warp_step(strip, carry):
            blend(strip, row, *corners(strip, row))
            return carry

        lax.fori_loop(0, strips, sums_step, 0, unroll=16)
        lax.fori_loop(0, strips, warp_step, 0, unroll=4)
        return carry

    pl.when(me < last)(functools.partial(count, edge_recv_sem.at[0], 2 * strips, RADIUS))
    pl.when(me > 0)(functools.partial(count, edge_recv_sem.at[1], 2 * strips, RADIUS))

    def edge_step(strip, carry):
        row_sums(strip, 0)
        sums_of_three(strip, 0)
        row_sums(strip, band)
        return carry

    lax.fori_loop(0, strips, edge_step, 0, unroll=2)
    lax.fori_loop(0, band // GROUP - 2, group_step, 0)

    last_rows = band - GROUP
    last_groups = (band - 2 * GROUP, band - GROUP)

    def moving_step(strip, carry):
        row_sums_of_moving(strip, last_rows)
        return carry

    def corner_step(strip, carry):
        for group, row in enumerate(last_groups):
            for place, value in enumerate(corners(strip, row)):
                corner_buf[group, place, strip] = value
        return carry

    def fixed_step(strip, carry):
        row_sums_with_fixed(strip, last_rows)
        sums_of_three(strip, last_rows)
        sums_of_three(strip, band)
        return carry

    def blend_step(strip, carry):
        for group, row in enumerate(last_groups):
            blend(strip, row, *(corner_buf[group, place, strip] for place in range(4)))
        return carry

    count(recv_sem.at[chunks - 1], blocks // 2, chunk_rows(chunks - 1))
    lax.fori_loop(0, strips, moving_step, 0, unroll=8)
    lax.fori_loop(0, strips, corner_step, 0, unroll=2)
    count(recv_sem.at[chunks], blocks // 2, chunk_rows(chunks - 1))
    lax.fori_loop(0, strips, fixed_step, 0, unroll=16)
    lax.fori_loop(0, strips, blend_step, 0, unroll=4)

    pl.when(me > 0)(functools.partial(count, edge_send_sem.at[0], 2 * strips, RADIUS))
    pl.when(me < last)(functools.partial(count, edge_send_sem.at[1], 2 * strips, RADIUS))
    for chunk in range(chunks - 1):
        count(send_sem.at[chunk], blocks, chunk_rows(chunk))
    for place in (chunks - 1, chunks):
        count(send_sem.at[place], blocks // 2, chunk_rows(chunks - 1))


def solution(mesh):
    strips = mesh.shape["tile"]

    def on_device(fixed, moving, offsets, fractions):
        band, width = offsets.shape[1:]
        padded = band + 2 * RADIUS + 2 * GROUP
        chunks = len(CHUNKS)
        return pl.pallas_call(
            functools.partial(kernel, strips),
            out_shape=pltpu.VMEM((band, width), jnp.float32),
            in_specs=[pl.BlockSpec(memory_space=pltpu.HBM)] * 4,
            out_specs=pl.BlockSpec(memory_space=pltpu.VMEM),
            scratch_shapes=[
                pltpu.VMEM((2 * (strips + 2), padded, LANES), jnp.float32),
                pltpu.VMEM((strips, len(KEPT_SHIFTS), padded, LANES), jnp.float32),
                pltpu.VMEM((strips, 5, padded, LANES), jnp.float32),
                pltpu.VMEM((strips, 5, padded, LANES), jnp.float32),
                pltpu.VMEM(offsets.shape, offsets.dtype),
                pltpu.VMEM(fractions.shape, fractions.dtype),
                pltpu.SemaphoreType.DMA((chunks + 1,)),
                pltpu.SemaphoreType.DMA((chunks + 1,)),
                pltpu.SemaphoreType.DMA((4,)),
                pltpu.SemaphoreType.REGULAR((3,)),
                pltpu.SemaphoreType.DMA((2,)),
                pltpu.SemaphoreType.DMA((2,)),
                pltpu.VMEM((2, 4, strips, GROUP, LANES), jnp.float32),
            ],
            compiler_params=pltpu.CompilerParams(
                collective_id=0, has_side_effects=True, vmem_limit_bytes=60 * 2**20
            ),
        )(fixed, moving, offsets, fractions)

    placed = (
        P("pair", "tile"),
        P("pair", "tile"),
        P(None, ("pair", "tile"), None),
        P(None, ("pair", "tile"), None),
    )
    return jax.shard_map(
        on_device, mesh=mesh, in_specs=placed, out_specs=P(("pair", "tile"), None), check_vma=False
    )
```

time: 57.9 us -> 57.3 us (0.990)
  Pallas kernels: 56.7 us -> 55.7 us
    pallas_call x1, Pallas kernels: 56.7 us -> 55.7 us  [on_device(): pl.pallas_call(functools.partial(kernel, strips), out_shape=pltpu.VMEM((b...]
where the time goes in v5:
time: 57.3 us; the launch traced here: 56.7 us
  Pallas kernels  55.7 us (97%)
  local copies, waits for them, and re-layouts  0.97 us (2%)
    pallas_call x1, Pallas kernels, on_device(): pl.pallas_call(functools.partial(kernel, strips), out_shape=pltpu.VMEM((b...  55.7 us

profile of v5, /device:TPU:36, one launch (start us, length us, event | category | flops | bytes accessed | tf_op | source)
XLA Modules:
  0.0 56.7 jit_solution(12699155811066714401)
XLA Ops:
  0.0 55.7 %shard_map.46 = f32[128,2048]{1,0:T(8,128)S(1)} custom-call(f32[2048,128]{1,0:T(8,128)} %fixed_ref.1, f32[2048,128]{1,0:T(8,128)} %moving_ref.1, s32[2,128,2048]{2,1,0:T(8,128)} %offsets_ref.1, f32[2,128,2048]{2,1,0:T(8,128)} %fractions_ref.1), custom_call_target="tpu_custom_call" | custom-call | tf_op jit(solution)/shard_map/pallas_call | solution.py:384
  55.7 1.0 %copy.6 = f32[128,2048]{1,0:T(8,128)} copy(f32[128,2048]{1,0:T(8,128)S(1)} %shard_map.46) | data formatting | bytes 2097152

commit v6 on v5

--- a/solution.py
+++ b/solution.py
@@ -360,11 +360,11 @@
         return carry
 
     count(recv_sem.at[chunks - 1], blocks // 2, chunk_rows(chunks - 1))
-    lax.fori_loop(0, strips, moving_step, 0, unroll=8)
-    lax.fori_loop(0, strips, corner_step, 0, unroll=2)
+    lax.fori_loop(0, strips, moving_step, 0, unroll=16)
+    lax.fori_loop(0, strips, corner_step, 0, unroll=4)
     count(recv_sem.at[chunks], blocks // 2, chunk_rows(chunks - 1))
     lax.fori_loop(0, strips, fixed_step, 0, unroll=16)
-    lax.fori_loop(0, strips, blend_step, 0, unroll=4)
+    lax.fori_loop(0, strips, blend_step, 0, unroll=8)
 
     pl.when(me > 0)(functools.partial(count, edge_send_sem.at[0], 2 * strips, RADIUS))
     pl.when(me < last)(functools.partial(count, edge_send_sem.at[1], 2 * strips, RADIUS))

time: 57.3 us -> 57.1 us (level)
  no operation moved by 1% of the time
where the time goes in v6:
time: 57.1 us; the launch traced here: 56.7 us
  Pallas kernels  55.7 us (98%)
  local copies, waits for them, and re-layouts  0.97 us (2%)
    pallas_call x1, Pallas kernels, on_device(): pl.pallas_call(functools.partial(kernel, strips), out_shape=pltpu.VMEM((b...  55.7 us

profile of v6, /device:TPU:36, one launch (start us, length us, event | category | flops | bytes accessed | tf_op | source)
XLA Modules:
  0.0 56.7 jit_solution(5229915749374838599)
XLA Ops:
  0.0 55.7 %shard_map.46 = f32[128,2048]{1,0:T(8,128)S(1)} custom-call(f32[2048,128]{1,0:T(8,128)} %fixed_ref.1, f32[2048,128]{1,0:T(8,128)} %moving_ref.1, s32[2,128,2048]{2,1,0:T(8,128)} %offsets_ref.1, f32[2,128,2048]{2,1,0:T(8,128)} %fractions_ref.1), custom_call_target="tpu_custom_call" | custom-call | tf_op jit(solution)/shard_map/pallas_call | solution.py:384
  55.7 1.0 %copy.6 = f32[128,2048]{1,0:T(8,128)} copy(f32[128,2048]{1,0:T(8,128)S(1)} %shard_map.46) | data formatting | bytes 2097152
